TPU v7x, 512 devices: a whole 4x8x8 slice. The times are simulated.
512 devices in a mesh: row: 16 (over x_lo, z), col: 32 (over y, x_hi, core).
Axes of the slice: x: 4 (x_hi: 2, x_lo: 2; x = x_hi * 2 + x_lo), y: 8, z: 8, core: 2. Of those that a mesh axis runs over, the one named last changes fastest.
Arguments:
- layer_input: bfloat16 [256, 8192], P('col', 'row'), may hold values from -6 to 6
- out_grad: bfloat16 [256, 8192], P('col', 'row'), may hold values from -6 to 6
- gate_weight: bfloat16 [8192, 28672], P('row', 'col'), may hold values from -0.0625 to 0.0625
- up_weight: bfloat16 [8192, 28672], P('row', 'col'), may hold values from -0.0625 to 0.0625
- down_weight: bfloat16 [28672, 8192], P('col', 'row'), may hold values from -0.03125 to 0.03125
Outputs:
- input_grad: bfloat16 [256, 8192], P('col', 'row')
- down_grad: bfloat16 [28672, 8192], P('col', 'row')
All inputs are finite; a program needn't handle non-finite values.
Results may differ from a plain program's by a relative error of at most 0.0049.
Values may be sent and summed in bfloat16 or wider, within the bound.
A program may use at most 64 MiB of HBM per device.

v0:
```python
import jax
import jax.numpy as jnp
from jax import lax
from jax.sharding import PartitionSpec as P


def in_one_piece(arrays, axis, dim, along):
    both = jnp.concatenate(arrays, axis=along)
    whole, at, done = (lax.all_gather(both, axis, axis=dim, tiled=True), 0, [])
    for a in arrays:
        done.append(lax.slice_in_dim(whole, at, at + a.shape[along], axis=along))
        at += a.shape[along]
    return tuple(done)


def in_blocks(x, dim, size):
    before, after = (x.shape[:dim], x.shape[dim + 1 :])
    return jnp.moveaxis(x.reshape(*before, size, -1, *after), dim, 0)


def sent_and_summed(x, axis, dim):
    size = lax.axis_size(axis)
    pieces = lax.all_to_all(in_blocks(x, dim, size), axis, 0, 0, tiled=True)
    return jnp.sum(pieces, axis=0)


def sent_together(arrays, axis, dim, along):
    ends, at = ([], 0)
    for a in arrays[:-1]:
        at += a.shape[along]
        ends.append(at)
    both = jnp.concatenate(arrays, axis=along)
    return tuple(jnp.split(sent_and_summed(both, axis, dim), ends, axis=along))


def copy_for_each(x, axis):
    size = lax.axis_size(axis)
    return lax.all_to_all(jnp.broadcast_to(x[None], (size, *x.shape)), axis, 0, 0, tiled=True)


def joined_along(pieces, dim):
    lengths = list(pieces.shape[1:])
    lengths[dim] *= pieces.shape[0]
    return jnp.moveaxis(pieces, 0, dim).reshape(lengths)


def gather_directly(x, axis, dim):
    pieces = copy_for_each(x, axis)
    return joined_along(pieces, dim)


def in_one_piece_2(arrays, axis, dim, along):
    ends, at = ([], 0)
    for a in arrays[:-1]:
        at += a.shape[along]
        ends.append(at)
    both = jnp.concatenate(arrays, axis=along)
    return tuple(jnp.split(gather_directly(both, axis, dim), ends, axis=along))


def swiglu_back(gate, up, hidden_grad):
    sig = jax.nn.sigmoid(gate)
    silu = gate * sig
    hidden = (silu * up).astype(jnp.bfloat16)
    up_grad = (hidden_grad * silu).astype(jnp.bfloat16)
    gate_grad = (hidden_grad * up * sig * (1.0 + gate * (1.0 - sig))).astype(jnp.bfloat16)
    return (hidden, gate_grad, up_grad)


def contract_last(left, right):
    return lax.dot_general(
        left, right, (((1,), (1,)), ((), ())), preferred_element_type=jnp.float32
    )


def body(layer_input, out_grad, gate_weight, up_weight, down_weight):
    tokens, grads = in_one_piece((layer_input, out_grad), "col", 0, 1)
    gate_part = jnp.dot(tokens, gate_weight, preferred_element_type=jnp.float32)
    up_part = jnp.dot(tokens, up_weight, preferred_element_type=jnp.float32)
    grad_part = contract_last(grads, down_weight)
    gate, up, hidden_grad = sent_together((gate_part, up_part, grad_part), "row", 0, 1)
    hidden, gate_grad, up_grad = swiglu_back(gate, up, hidden_grad)
    hidden, gate_grad, up_grad = in_one_piece_2((hidden, gate_grad, up_grad), "row", 0, 1)
    down_grad = lax.dot_general(
        hidden, grads, (((0,), (0,)), ((), ())), preferred_element_type=jnp.float32
    ).astype(jnp.bfloat16)
    input_grad = sent_and_summed(
        contract_last(gate_grad, gate_weight) + contract_last(up_grad, up_weight), "col", 0
    )
    return (input_grad.astype(jnp.bfloat16), down_grad)


def solution(mesh):
    return jax.shard_map(
        body,
        mesh=mesh,
        in_specs=(
            P("col", "row"),
            P("col", "row"),
            P("row", "col"),
            P("row", "col"),
            P("col", "row"),
        ),
        out_specs=(P("col", "row"), P("col", "row")),
        check_vma=False,
    )
```

profile of v0, /device:TPU:1, one launch (start us, length us, event | category | flops | bytes accessed | tf_op | source)
XLA Modules:
  0.0 189.3 jit_solution(1724233101879965480)
XLA Ops:
  0.6 0.0 copy-start
  0.6 0.0 copy-start.2
  0.7 0.8 pad_maximum_fusion.2
  1.5 45.0 %all_gather.3 = bf16[256,1024]{1,0:T(8,128)(2,1)S(1)} all-gather(bf16[8,1024]{1,0:T(8,128)(2,1)S(1)} %pad_maximum_fusion.2), channel_id=1, replica_groups=mesh['row'=16,'col'=32] {'col'}, dimensions={0}, use_global_device_ids=true | all-gather | bytes 540672 | tf_op jit(solution)/shard_map/all_gather | solution.py:9
  46.5 1.6 fusion.8
  48.1 0.0 copy-done.2
  48.1 0.5 fusion.6
  48.6 0.0 copy-done
  48.6 0.4 fusion.10
  49.1 0.2 pad_maximum_fusion
  49.3 73.1 %all_to_all.15 = f32[16,16,2688]{2,1,0:T(8,128)} all-to-all(f32[16,16,2688]{2,1,0:T(8,128)S(1)} %bitcast.9), channel_id=1, replica_groups=mesh['row'=16,'col'=32] {'row'}, dimensions={0} | all-to-all | bytes 5505024 | tf_op jit(solution)/shard_map/all_to_all | solution.py:23
  122.3 1.9 %reduce_sum.18 = f32[16,2688]{1,0:T(8,128)S(1)} reduce(f32[16,16,2688]{2,1,0:T(8,128)} %all_to_all.15, f32[]{:T(128)} %constant.0.clone.1), dimensions={0}, to_apply=%region_0.0 | reduce | flops 645120 | bytes 2924548 | tf_op jit(solution)/shard_map/reduce_sum | solution.py:24
  124.3 0.1 broadcast_in_dim.2
  124.4 0.0 copy-start.1
  124.4 37.8 %all_to_all.16 = bf16[16,16,2688]{2,1,0:T(8,128)(2,1)S(1)} all-to-all(bf16[16,16,2688]{2,1,0:T(8,128)(2,1)S(1)} %broadcast_in_dim.2), channel_id=1, replica_groups=mesh['row'=16,'col'=32] {'row'}, dimensions={0} | all-to-all | bytes 2752512 | tf_op jit(solution)/shard_map/all_to_all | solution.py:38
  162.2 0.5 fusion.3
  162.7 0.0 copy-done.1
  162.7 1.3 fusion
  163.9 7.8 %all-to-all-start.2 = ((f32[32,8,512]{2,1,0:T(8,128)}), f32[32,8,512]{2,1,0:T(8,128)S(1)}, u32[]{:S(2)}, u32[]{:S(2)}) async-start(f32[32,8,512]{2,1,0:T(8,128)} %fusion), calls=%async_computation.2 | async-start | bytes 1048576 | tf_op jit(solution)/shard_map/all_to_all | solution.py:23
  171.8 1.4 convolution_convert_fusion
  173.1 15.5 %all-to-all-done.2 = f32[32,8,512]{2,1,0:T(8,128)S(1)} async-done(((f32[32,8,512]{2,1,0:T(8,128)}), f32[32,8,512]{2,1,0:T(8,128)S(1)}, u32[]{:S(2)}, u32[]{:S(2)}) %all-to-all-start.2) | async-done | bytes 524320 | tf_op jit(solution)/shard_map/all_to_all | solution.py:23
  188.6 0.6 reduce_sum.19
  (2 shorter events, 0.1 us)
Async XLA Ops:
  0.6 48.0 %copy-start = (bf16[512,896]{1,0:T(8,128)(2,1)S(1)}, bf16[512,896]{1,0:T(8,128)(2,1)}, u32[]{:S(2)}) copy-start(bf16[512,896]{1,0:T(8,128)(2,1)} %param.7) | copy-start | bytes 2752516
  0.6 47.5 %copy-start.2 = (bf16[896,512]{1,0:T(8,128)(2,1)S(1)}, bf16[896,512]{1,0:T(8,128)(2,1)}, u32[]{:S(2)}) copy-start(bf16[896,512]{1,0:T(8,128)(2,1)} %param.9) | copy-start | bytes 2752516
  124.4 38.3 %copy-start.1 = (bf16[512,896]{1,0:T(8,128)(2,1)S(1)}, bf16[512,896]{1,0:T(8,128)(2,1)}, u32[]{:S(2)}) copy-start(bf16[512,896]{1,0:T(8,128)(2,1)} %param.8) | copy-start | bytes 2752516
  163.9 24.7 %all-to-all-start.2 = ((f32[32,8,512]{2,1,0:T(8,128)}), f32[32,8,512]{2,1,0:T(8,128)S(1)}, u32[]{:S(2)}, u32[]{:S(2)}) async-start(f32[32,8,512]{2,1,0:T(8,128)} %fusion), calls=%async_computation.2 | async-start | bytes 1048576 | tf_op jit(solution)/shard_map/all_to_all | solution.py:23
where the time goes:
time: 190 us; the launch traced here: 189 us
  blocking collectives  156 us (82%)
  waiting for transfers between devices  15.5 us (8%)
  starting transfers between devices  7.8 us (4%)
  matrix products  5.58 us (3%)
  other arithmetic  3.65 us (2%)
    all_to_all x1, blocking collectives, sent_and_summed(): pieces = lax.all_to_all(in_blocks(x, dim, size), axis, 0, 0, tiled=True)  73.1 us
    all_gather x1, blocking collectives, in_one_piece(): whole, at, done = (lax.all_gather(both, axis, axis=dim, tiled=True), 0, [])  45 us
    all_to_all x1, blocking collectives, copy_for_each(): lax.all_to_all(jnp.broadcast_to(x[None], (size, *x.shape)), axis, 0, 0, t...  37.8 us
    all_to_all x1, waiting for transfers between devices, sent_and_summed(): pieces = lax.all_to_all(in_blocks(x, dim, size), axis, 0, 0, tiled=True)  15.5 us
    all_to_all x1, starting transfers between devices, sent_and_summed(): pieces = lax.all_to_all(in_blocks(x, dim, size), axis, 0, 0, tiled=True)  7.8 us
  transfers between devices with their start and end apart: 1, of which 1 were waited for; matrix products, arithmetic and copies ran while one was open for 1% of the time, Pallas kernels for 0%

commit v1 on v0

v1 whole, which is shorter than its diff:
```python
import functools

import jax
import jax.numpy as jnp
from jax import lax
from jax.experimental import pallas as pl
from jax.experimental.pallas import tpu as pltpu
from jax.sharding import PartitionSpec as P

MESH = pl.DeviceIdType.MESH
WIDTHS = (256, 256, 256, 128)
OFFS = (0, 256, 512, 768)
G = len(WIDTHS)
BF16_HOPS = 2
NZ, NY, NX = 8, 8, 2
F32 = jnp.float32
BF16 = jnp.bfloat16


def contract_last(left, right):
    return lax.dot_general(
        left, right, (((1,), (1,)), ((), ())), preferred_element_type=F32
    )


def contract_first(left, right):
    return lax.dot_general(
        left, right, (((0,), (0,)), ((), ())), preferred_element_type=F32
    )


def remote(src, dst, send_sem, recv_sem, row, col):
    return pltpu.make_async_remote_copy(
        src_ref=src,
        dst_ref=dst,
        send_sem=send_sem,
        recv_sem=recv_sem,
        device_id={"row": row, "col": col},
        device_id_type=MESH,
    )


def kernel(li, og, wg_hbm, wu_hbm, wd_hbm, ig_out, dg_out, *scratch):
    scratch = list(scratch)
    take = lambda n: [scratch.pop(0) for _ in range(n)]
    (xg, wg, wu, wd) = take(4)
    part = take(G)
    sent = take(G)
    got16 = take(G)
    got32 = take(G)
    xsend = take(G)
    xrecv = take(G)
    full = take(G)
    (igs, core_got, chip_sent, chip_got) = take(4)
    (local_sem, a_send, a_recv, f_send, f_recv) = take(5)
    (rs_send, rs_recv, x_send, x_recv, ag_send, ag_recv) = take(6)
    (c_send, c_recv, d_send, d_recv) = take(4)

    row = lax.axis_index("row")
    col = lax.axis_index("col")
    z = lax.rem(row, NZ)
    x_lo = row // NZ
    core = lax.rem(col, 2)
    x_hi = lax.rem(col // 2, 2)
    y = col // 4
    s = 1 - 2 * core
    mod8 = lambda v: lax.rem(v + 16, 8)
    ahead = x_lo * NZ + mod8(z + s)
    behind = x_lo * NZ + mod8(z - s)
    across = (1 - x_lo) * NZ + z
    partner = col + s

    steps = [(dy, dx) for dy in (4, 3, 5, 2, 6, 1, 7, 0) for dx in (1, 0)][:-1]

    def chip_at(dy, dx):
        return mod8(y + dy) * 4 + lax.rem(x_hi + dx, 2) * 2

    loads = [
        pltpu.make_async_copy(
            li, xg.at[pl.ds(pl.multiple_of(col * 8, 8), 8), pl.ds(0, 512)], local_sem.at[0]
        ),
        pltpu.make_async_copy(
            og, xg.at[pl.ds(pl.multiple_of(col * 8, 8), 8), pl.ds(512, 512)], local_sem.at[1]
        ),
        pltpu.make_async_copy(wg_hbm, wg, local_sem.at[2]),
        pltpu.make_async_copy(wu_hbm, wu, local_sem.at[3]),
        pltpu.make_async_copy(wd_hbm, wd, local_sem.at[4]),
    ]
    for load in loads:
        load.start()

    barrier = pltpu.get_barrier_semaphore()
    greet = [(row, chip_at(dy, dx) + core) for dy, dx in steps]
    greet += [(row, partner), (ahead, col), (behind, col), (across, col)]
    for r, c in greet:
        pl.semaphore_signal(
            barrier, inc=1, device_id={"row": r, "col": c}, device_id_type=MESH
        )
    pl.semaphore_wait(barrier, len(greet))

    pending = []

    def go(copy):
        copy.start()
        pending.append(copy)
        return copy

    def rows_of(c):
        return xg.at[pl.ds(pl.multiple_of(c * 8, 8), 8), :]

    loads[0].wait()
    loads[1].wait()
    for i, (dy, dx) in enumerate(steps):
        go(remote(rows_of(col), rows_of(col), a_send.at[i], a_recv.at[i], row, chip_at(dy, dx) + core))
    go(remote(rows_of(col), rows_of(col), f_send.at[15], f_recv.at[15], row, partner))
    for i in reversed(range(15)):
        dy, dx = steps[i]
        src = chip_at(-dy, dx)
        remote(rows_of(src + core), rows_of(src + core), a_send.at[i], a_recv.at[i], row, col).wait_recv()
        go(remote(rows_of(src + core), rows_of(src + core), f_send.at[i], f_recv.at[i], row, partner))
    for i in reversed(range(16)):
        src = chip_at(-steps[i][0], steps[i][1]) + 1 - core if i < 15 else partner
        remote(rows_of(src), rows_of(src), f_send.at[i], f_recv.at[i], row, partner).wait_recv()
    for load in loads[2:]:
        load.wait()

    tokens = xg[:, 0:512]
    grads = xg[:, 512:1024]

    def long_copy(g, k, chunk):
        if k <= BF16_HOPS:
            src, dst = sent[g].at[0, k - 1], got16[g].at[0, k - 1]
        else:
            src, dst = part[g].at[chunk], got32[g].at[k - 3]
        return remote(src, dst, rs_send.at[g, 0, k - 1], rs_recv.at[g, 0, k - 1], ahead, col)

    def short_copy(g, k, chunk):
        if k <= BF16_HOPS:
            src, dst = sent[g].at[1, k - 1], got16[g].at[1, k - 1]
        else:
            src, dst = part[g].at[chunk], got32[g].at[2]
        return remote(src, dst, rs_send.at[g, 1, k - 1], rs_recv.at[g, 1, k - 1], behind, col)

    for g in range(G):
        w, cols = WIDTHS[g], pl.ds(OFFS[g], WIDTHS[g])
        part[g][:, 0] = jnp.dot(tokens, wg[:, cols], preferred_element_type=F32).reshape(8, 32, w)
        part[g][:, 1] = jnp.dot(tokens, wu[:, cols], preferred_element_type=F32).reshape(8, 32, w)
        part[g][:, 2] = contract_last(grads, wd[cols, :]).reshape(8, 32, w)
        far, near = mod8(z + 4 * s), mod8(z - 3 * s)
        sent[g][0, 0] = part[g][far].astype(BF16)
        go(long_copy(g, 1, far))
        sent[g][1, 0] = part[g][near].astype(BF16)
        go(short_copy(g, 1, near))
    for k in (2, 3, 4):
        for g in range(G):
            chunk = mod8(z + (5 - k) * s)
            long_copy(g, k - 1, chunk).wait_recv()
            if k - 1 <= BF16_HOPS:
                value = got16[g][0, k - 2].astype(F32) + part[g][chunk]
            else:
                value = got32[g][k - 4] + part[g][chunk]
            if k <= BF16_HOPS:
                sent[g][0, k - 1] = value.astype(BF16)
            else:
                part[g][chunk] = value
            go(long_copy(g, k, chunk))
            if k < 4:
                chunk = mod8(z - (4 - k) * s)
                short_copy(g, k - 1, chunk).wait_recv()
                value = got16[g][1, k - 2].astype(F32) + part[g][chunk]
                if k <= BF16_HOPS:
                    sent[g][1, k - 1] = value.astype(BF16)
                else:
                    part[g][chunk] = value
                go(short_copy(g, k, chunk))

    def x_copy(g):
        return remote(xsend[g], xrecv[g], x_send.at[g], x_recv.at[g], across, col)

    def gather_copy(g, flow, k, chunk):
        return remote(
            full[g].at[chunk],
            full[g].at[chunk],
            ag_send.at[g, flow, k - 1],
            ag_recv.at[g, flow, k - 1],
            (ahead, behind)[flow],
            col,
        )

    def finish(g):
        long_copy(g, 4, z).wait_recv()
        short_copy(g, 3, z).wait_recv()
        xsend[g][...] = part[g][z] + got32[g][1] + got32[g][2]
        go(x_copy(g))

    def middle(g):
        x_copy(g).wait_recv()
        gate = xsend[g][0] + xrecv[g][0]
        up = xsend[g][1] + xrecv[g][1]
        hidden_grad = xsend[g][2] + xrecv[g][2]
        sig = jax.nn.sigmoid(gate)
        silu = gate * sig
        full[g][z, 0] = (silu * up).astype(BF16)
        full[g][z, 1] = (hidden_grad * up * sig * (1.0 + gate * (1.0 - sig))).astype(BF16)
        full[g][z, 2] = (hidden_grad * silu).astype(BF16)
        go(gather_copy(g, 0, 1, z))
        go(gather_copy(g, 1, 1, z))

    LAG = 2
    for i in range(G + LAG):
        if i < G:
            finish(i)
        if i >= LAG:
            middle(i - LAG)
    for k in (2, 3, 4):
        for g in range(G):
            chunk = mod8(z - (k - 1) * s)
            gather_copy(g, 0, k - 1, chunk).wait_recv()
            go(gather_copy(g, 0, k, chunk))
            if k < 4:
                chunk = mod8(z + (k - 1) * s)
                gather_copy(g, 1, k - 1, chunk).wait_recv()
                go(gather_copy(g, 1, k, chunk))

    total = None
    for g in range(G):
        gather_copy(g, 1, 3, mod8(z + 3 * s)).wait_recv()
        gather_copy(g, 0, 4, mod8(z - 4 * s)).wait_recv()
        w, cols = WIDTHS[g], pl.ds(OFFS[g], WIDTHS[g])
        term = contract_last(full[g][:, 1].reshape(256, w), wg[:, cols])
        term += contract_last(full[g][:, 2].reshape(256, w), wu[:, cols])
        total = term if total is None else total + term
    igs[...] = total.reshape(16, 2, 8, 512)

    core_copy = go(
        remote(igs.at[:, 1 - core], core_got, c_send.at[0], c_recv.at[0], row, partner)
    )

    def weight_grad(g):
        w, cols = WIDTHS[g], pl.ds(OFFS[g], WIDTHS[g])
        dg_out[cols, :] = contract_first(full[g][:, 0].reshape(256, w), grads).astype(BF16)

    weight_grad(0)
    core_copy.wait_recv()
    both = igs[:, core] + core_got[...]
    core_got[...] = both
    chip_sent[...] = both.astype(BF16)
    for i, (dy, dx) in enumerate(steps):
        chip = chip_at(dy, dx)
        go(
            remote(
                chip_sent.at[chip // 2], chip_got.at[i], d_send.at[i], d_recv.at[i], row, chip + core
            )
        )
    for g in range(1, G):
        weight_grad(g)
    done = core_got[col // 2]
    for i in reversed(range(15)):
        remote(chip_sent.at[0], chip_got.at[i], d_send.at[i], d_recv.at[i], row, col).wait_recv()
        done += chip_got[i].astype(F32)
    ig_out[...] = done.astype(BF16)

    for copy in pending:
        copy.wait_send()


def body(layer_input, out_grad, gate_weight, up_weight, down_weight):
    dma = pltpu.SemaphoreType.DMA
    chunks = lambda lead, kind: [pltpu.VMEM((*lead, 3, 32, w), kind) for w in WIDTHS]
    scratch = [
        pltpu.VMEM((256, 1024), BF16),
        pltpu.VMEM((512, 896), BF16),
        pltpu.VMEM((512, 896), BF16),
        pltpu.VMEM((896, 512), BF16),
        *chunks((8,), F32),
        *chunks((2, BF16_HOPS), BF16),
        *chunks((2, BF16_HOPS), BF16),
        *chunks((3,), F32),
        *chunks((), F32),
        *chunks((), F32),
        *chunks((8,), BF16),
        pltpu.VMEM((16, 2, 8, 512), F32),
        pltpu.VMEM((16, 8, 512), F32),
        pltpu.VMEM((16, 8, 512), BF16),
        pltpu.VMEM((15, 8, 512), BF16),
        dma((5,)),
        dma((15,)),
        dma((15,)),
        dma((16,)),
        dma((16,)),
        dma((G, 2, 4)),
        dma((G, 2, 4)),
        dma((G,)),
        dma((G,)),
        dma((G, 2, 4)),
        dma((G, 2, 4)),
        dma((1,)),
        dma((1,)),
        dma((15,)),
        dma((15,)),
    ]
    hbm = pl.BlockSpec(memory_space=pl.ANY)
    vmem = pl.BlockSpec(memory_space=pltpu.VMEM)
    return pl.pallas_call(
        kernel,
        out_shape=(
            jax.ShapeDtypeStruct((8, 512), BF16),
            jax.ShapeDtypeStruct((896, 512), BF16),
        ),
        in_specs=[hbm] * 5,
        out_specs=(vmem, vmem),
        scratch_shapes=scratch,
        compiler_params=pltpu.CompilerParams(
            collective_id=0, has_side_effects=True, vmem_limit_bytes=60 * 1024 * 1024
        ),
        name="swiglu_back",
    )(layer_input, out_grad, gate_weight, up_weight, down_weight)


def solution(mesh):
    return jax.shard_map(
        body,
        mesh=mesh,
        in_specs=(
            P("col", "row"),
            P("col", "row"),
            P("row", "col"),
            P("row", "col"),
            P("col", "row"),
        ),
        out_specs=(P("col", "row"), P("col", "row")),
        check_vma=False,
    )
```

time: 190 us -> 82.8 us (0.44)
  blocking collectives: 156 us -> 0 us
  Pallas kernels: 0 us -> 78.5 us
  waiting for transfers between devices: 15.5 us -> 0 us
  starting transfers between devices: 7.8 us -> 0 us
  matrix products: 5.58 us -> 0 us
  other arithmetic: 3.65 us -> 0 us
  local copies, waits for them, and re-layouts: 0.11 us -> 3.46 us
    all_to_all x2 -> x0, blocking collectives: 111 us -> none  [the longest x1 73.1 us: sent_and_summed(): pieces = lax.all_to_all(in_blocks(x, dim, size), axis, 0, 0, tiled=True)]
    pallas_call x0 -> x1, Pallas kernels: none -> 78.5 us  [body(): pl.pallas_call(kernel, out_shape=(jax.ShapeDtypeStruct((8, 512), BF16), j...]
    all_gather x1 -> x0, blocking collectives: 45 us -> none  [in_one_piece(): whole, at, done = (lax.all_gather(both, axis, axis=dim, tiled=True), 0, [])]
    all_to_all x1 -> x0, waiting for transfers between devices: 15.5 us -> none  [sent_and_summed(): pieces = lax.all_to_all(in_blocks(x, dim, size), axis, 0, 0, tiled=True)]
    all_to_all x1 -> x0, starting transfers between devices: 7.8 us -> none  [sent_and_summed(): pieces = lax.all_to_all(in_blocks(x, dim, size), axis, 0, 0, tiled=True)]
    dot_general x6 -> x0, matrix products: 5.58 us -> none  [the longest x3 2.19 us: contract_last(): lax.dot_general(left, right, (((1,), (1,)), ((), ())), preferred_element_...]
    unnamed x6 -> x2, local copies, waits for them, and re-layouts: 0.02 us -> 3.46 us
    reduce_sum x2 -> x0, other arithmetic: 2.56 us -> none  [sent_and_summed(): return jnp.sum(pieces, axis=0)]
  transfers between devices with their start and end apart: 1 -> 0, of which waited for: 1 -> 0; matrix products, arithmetic and copies ran while one was open for 1% -> 0% of each run, Pallas kernels for 0% -> 0%
where the time goes in v1:
time: 82.8 us; the launch traced here: 82.6 us
  Pallas kernels  78.5 us (95%)
  local copies, waits for them, and re-layouts  3.46 us (4%)
    pallas_call x1, Pallas kernels, body(): pl.pallas_call(kernel, out_shape=(jax.ShapeDtypeStruct((8, 512), BF16), j...  78.5 us
    unnamed x2, local copies, waits for them, and re-layouts  3.46 us

profile of v1, /device:TPU:1, one launch (start us, length us, event | category | flops | bytes accessed | tf_op | source)
XLA Modules:
  0.0 82.6 jit_solution(2227159481913347498)
XLA Ops:
  0.6 78.5 %swiglu_back.1 = (bf16[8,512]{1,0:T(8,128)(2,1)}, bf16[896,512]{1,0:T(8,128)(2,1)}) custom-call(bf16[8,512]{1,0:T(8,128)(2,1)} %li.1, bf16[8,512]{1,0:T(8,128)(2,1)} %og.1, bf16[512,896]{1,0:T(8,128)(2,1)} %wg_hbm.1, bf16[512,896]{1,0:T(8,128)(2,1)} %wu_hbm.1, bf16[896,512]{1,0:T(8,128)(2,1)} %wd_hbm.1), custom_call_target="tpu_custom_call" | custom-call | tf_op jit(solution)/shard_map/swiglu_back/pallas_call | solution.py:304
  79.1 1.3 %copy.9 = bf16[8,512]{1,0:T(8,128)(2,1)} copy(bf16[8,512]{1,0:T(8,128)(2,1)} %get-tuple-element.4) | data formatting | bytes 16384
  80.4 2.2 %copy.10 = bf16[896,512]{1,0:T(8,128)(2,1)} copy(bf16[896,512]{1,0:T(8,128)(2,1)} %get-tuple-element.5) | data formatting | bytes 1835008

commit v2 on v1

v2 whole, which is shorter than its diff:
```python
import jax
import jax.numpy as jnp
from jax import lax
from jax.experimental import pallas as pl
from jax.experimental.pallas import tpu as pltpu
from jax.sharding import PartitionSpec as P

MESH = pl.DeviceIdType.MESH
WIDTHS = (256, 256, 256, 128)
OFFS = (0, 256, 512, 768)
G = len(WIDTHS)
NZ = 8
SIDE = (True, True, False, False)
FIRST = (True, False, False, False)
F32 = jnp.float32
BF16 = jnp.bfloat16


def contract_last(left, right):
    return lax.dot_general(
        left, right, (((1,), (1,)), ((), ())), preferred_element_type=F32
    )


def contract_first(left, right):
    return lax.dot_general(
        left, right, (((0,), (0,)), ((), ())), preferred_element_type=F32
    )


def early(g):
    return 1 if FIRST[g] else 2


def remote(src, dst, send_sem, recv_sem, row, col):
    return pltpu.make_async_remote_copy(
        src_ref=src,
        dst_ref=dst,
        send_sem=send_sem,
        recv_sem=recv_sem,
        device_id={"row": row, "col": col},
        device_id_type=MESH,
    )


def kernel(li, og, wg_hbm, wu_hbm, wd_hbm, ig_out, dg_out, *scratch):
    scratch = list(scratch)
    take = lambda n: [scratch.pop(0) for _ in range(n)]
    (xg, wg, wu, wd) = take(4)
    part = take(G)
    sent = take(G)
    got16 = take(G)
    got32 = take(G)
    xsend = take(G)
    xrecv = take(G)
    full = take(G)
    (igs, core_got, chip_sent, chip_got) = take(4)
    (local_sem, a_send, a_recv, f_send, f_recv) = take(5)
    (rs_send, rs_recv, x_send, x_recv, ag_send, ag_recv, side_send, side_recv) = take(8)
    (c_send, c_recv, d_send, d_recv) = take(4)

    row = lax.axis_index("row")
    col = lax.axis_index("col")
    z = lax.rem(row, NZ)
    x_lo = row // NZ
    core = lax.rem(col, 2)
    x_hi = lax.rem(col // 2, 2)
    y = col // 4
    s = 1 - 2 * core
    mod8 = lambda v: lax.rem(v + 16, 8)
    ahead = x_lo * NZ + mod8(z + s)
    behind = x_lo * NZ + mod8(z - s)
    across = (1 - x_lo) * NZ + z
    partner = col + s

    steps = [(dy, dx) for dy in (4, 3, 5, 2, 6, 1, 7, 0) for dx in (1, 0)][:-1]

    def chip_at(dy, dx):
        return mod8(y + dy) * 4 + lax.rem(x_hi + dx, 2) * 2

    loads = [
        pltpu.make_async_copy(
            li, xg.at[pl.ds(pl.multiple_of(col * 8, 8), 8), pl.ds(0, 512)], local_sem.at[0]
        ),
        pltpu.make_async_copy(
            og, xg.at[pl.ds(pl.multiple_of(col * 8, 8), 8), pl.ds(512, 512)], local_sem.at[1]
        ),
        pltpu.make_async_copy(wg_hbm, wg, local_sem.at[2]),
        pltpu.make_async_copy(wu_hbm, wu, local_sem.at[3]),
        pltpu.make_async_copy(wd_hbm, wd, local_sem.at[4]),
    ]
    for load in loads:
        load.start()

    barrier = pltpu.get_barrier_semaphore()
    greet = [(row, chip_at(dy, dx) + core) for dy, dx in steps]
    greet += [(row, partner), (ahead, col), (behind, col), (across, col)]
    for r, c in greet:
        pl.semaphore_signal(
            barrier, inc=1, device_id={"row": r, "col": c}, device_id_type=MESH
        )
    pl.semaphore_wait(barrier, len(greet))

    pending = []

    def go(copy):
        copy.start()
        pending.append(copy)
        return copy

    def rows_of(c):
        return xg.at[pl.ds(pl.multiple_of(c * 8, 8), 8), :]

    loads[0].wait()
    loads[1].wait()
    for i, (dy, dx) in enumerate(steps):
        go(remote(rows_of(col), rows_of(col), a_send.at[i], a_recv.at[i], row, chip_at(dy, dx) + core))
    go(remote(rows_of(col), rows_of(col), f_send.at[15], f_recv.at[15], row, partner))
    for i in reversed(range(15)):
        dy, dx = steps[i]
        src = chip_at(-dy, dx)
        remote(rows_of(src + core), rows_of(src + core), a_send.at[i], a_recv.at[i], row, col).wait_recv()
        go(remote(rows_of(src + core), rows_of(src + core), f_send.at[i], f_recv.at[i], row, partner))
    for i in reversed(range(16)):
        src = chip_at(-steps[i][0], steps[i][1]) + 1 - core if i < 15 else partner
        remote(rows_of(src), rows_of(src), f_send.at[i], f_recv.at[i], row, partner).wait_recv()
    for load in loads[2:]:
        load.wait()

    tokens = xg[:, 0:512]
    grads = xg[:, 512:1024]

    def part_ref(g, chunk):
        return part[g].at[x_lo, chunk] if FIRST[g] else part[g].at[chunk]

    def own(g, chunk):
        value = part_ref(g, chunk)[...]
        return value + xrecv[g][chunk].astype(F32) if FIRST[g] else value

    def ring_copy(g, flow, k, chunk):
        e = early(g)
        if k <= e:
            src, dst = sent[g].at[flow, k - 1], got16[g].at[flow, k - 1]
        else:
            src, dst = part_ref(g, chunk), got32[g].at[(k - e - 1) + flow * (4 - e)]
        return remote(
            src, dst, rs_send.at[g, flow, k - 1], rs_recv.at[g, flow, k - 1], (ahead, behind)[flow], col
        )

    def ring_got(g, flow, k):
        ring_copy(g, flow, k, z).wait_recv()
        e = early(g)
        if k <= e:
            return got16[g][flow, k - 1].astype(F32)
        return got32[g][(k - e - 1) + flow * (4 - e)]

    def products(g):
        w, cols = WIDTHS[g], pl.ds(OFFS[g], WIDTHS[g])
        for m in range(3):
            if m == 2:
                value = contract_last(grads, wd[cols, :])
            else:
                value = jnp.dot(tokens, (wg, wu)[m][:, cols], preferred_element_type=F32)
            if FIRST[g]:
                value = value.reshape(8, 2, 16, w)
                part[g][0, :, m] = value[:, 0]
                part[g][1, :, m] = value[:, 1]
            else:
                part[g][:, m] = value.reshape(8, 32, w)

    def ring_stage(g, k):
        for flow in (0, 1):
            if flow == 1 and k == 4:
                continue
            chunk = mod8(z + (5 - k) * s) if flow == 0 else mod8(z - (4 - k) * s)
            if k == 1:
                if FIRST[g]:
                    pair_copy(g, k - 1 + 4 * flow, chunk).wait_recv()
                value = own(g, chunk)
            else:
                if FIRST[g]:
                    pair_copy(g, k - 1 + 4 * flow, chunk).wait_recv()
                value = ring_got(g, flow, k - 1) + own(g, chunk)
            if k <= early(g):
                sent[g][flow, k - 1] = value.astype(BF16)
            elif k > 1 or FIRST[g]:
                part_ref(g, chunk)[...] = value
            go(ring_copy(g, flow, k, chunk))

    def pair_copy(g, i, chunk):
        return remote(xsend[g].at[chunk], xrecv[g].at[chunk], x_send.at[g, i], x_recv.at[g, i], across, col)

    def pair_stage(g):
        xsend[g][...] = part[g][1 - x_lo].astype(BF16)
        for i, chunk in ((0, 4), (4, -3), (1, 3), (5, -2), (2, 2), (6, -1), (3, 1), (7, 0)):
            go(pair_copy(g, i, mod8(z + chunk * s)))

    later = [g for g in range(G) if not FIRST[g]] + [g for g in range(G) if FIRST[g]]
    for g in range(G):
        products(g)
        if FIRST[g]:
            pair_stage(g)
        else:
            ring_stage(g, 1)
    for g in range(G):
        if FIRST[g]:
            ring_stage(g, 1)
    for k in (2, 3, 4):
        for g in later:
            ring_stage(g, k)

    def x_copy(g):
        src, dst = xsend[g], xrecv[g]
        if SIDE[g]:
            src, dst = src.at[1 - x_lo], dst.at[1 - x_lo]
        return remote(src, dst, x_send.at[g, 0], x_recv.at[g, 0], across, col)

    def gather_copy(g, flow, k, chunk):
        ref = full[g].at[chunk, x_lo] if SIDE[g] else full[g].at[chunk]
        return remote(ref, ref, ag_send.at[g, flow, k - 1], ag_recv.at[g, flow, k - 1], (ahead, behind)[flow], col)

    def side_copy(g, i, chunk, half):
        ref = full[g].at[chunk, half]
        return remote(ref, ref, side_send.at[g, i], side_recv.at[g, i], across, col)

    def finish(g):
        value = part[g][z] + ring_got(g, 0, 4) + ring_got(g, 1, 3)
        xsend[g][0] = value[:, 0:16]
        xsend[g][1] = value[:, 16:32]
        go(x_copy(g))

    def middle(g):
        mine = x_lo if SIDE[g] else slice(None)
        if FIRST[g]:
            pair_copy(g, 7, z).wait_recv()
            value = own(g, z) + ring_got(g, 0, 4) + ring_got(g, 1, 3)
        else:
            x_copy(g).wait_recv()
            value = xsend[g][mine] + xrecv[g][mine]
        gate, up, hidden_grad = (value[..., m, :, :] for m in range(3))
        sig = jax.nn.sigmoid(gate)
        silu = gate * sig
        full[g][z, mine, 0] = (silu * up).astype(BF16)
        full[g][z, mine, 1] = (hidden_grad * up * sig * (1.0 + gate * (1.0 - sig))).astype(BF16)
        full[g][z, mine, 2] = (hidden_grad * silu).astype(BF16)
        go(gather_copy(g, 0, 1, z))
        go(gather_copy(g, 1, 1, z))
        if SIDE[g]:
            go(side_copy(g, 0, z, x_lo))

    def forward(g, k):
        chunk = mod8(z - (k - 1) * s)
        gather_copy(g, 0, k - 1, chunk).wait_recv()
        if k < 5:
            go(gather_copy(g, 0, k, chunk))
        if SIDE[g] and k > 1:
            go(side_copy(g, k - 1, chunk, x_lo))
        if k < 5:
            chunk = mod8(z + (k - 1) * s)
            gather_copy(g, 1, k - 1, chunk).wait_recv()
            if k < 4:
                go(gather_copy(g, 1, k, chunk))
            if SIDE[g]:
                go(side_copy(g, k + 3, chunk, x_lo))

    for g in range(G):
        if not FIRST[g]:
            finish(g)
    for g in range(G):
        middle(g)
    for k in (2, 3, 4):
        for g in range(G):
            forward(g, k)
    for g in range(G):
        if SIDE[g]:
            forward(g, 5)

    def gathered(g, m):
        return full[g][:, :, m].reshape(256, WIDTHS[g])

    total = None
    for g in sorted(range(G), key=lambda g: SIDE[g]):
        if SIDE[g]:
            for i in range(8):
                chunk = mod8(z - i * s) if i < 5 else mod8(z + (i - 4) * s)
                side_copy(g, i, chunk, 1 - x_lo).wait_recv()
        else:
            forward(g, 5)
        w, cols = WIDTHS[g], pl.ds(OFFS[g], WIDTHS[g])
        term = contract_last(gathered(g, 1), wg[:, cols])
        term += contract_last(gathered(g, 2), wu[:, cols])
        total = term if total is None else total + term
    igs[...] = total.reshape(16, 2, 8, 512)

    core_copy = go(
        remote(igs.at[:, 1 - core], core_got, c_send.at[0], c_recv.at[0], row, partner)
    )

    def weight_grad(g):
        w, cols = WIDTHS[g], pl.ds(OFFS[g], WIDTHS[g])
        dg_out[cols, :] = contract_first(gathered(g, 0), grads).astype(BF16)

    weight_grad(0)
    core_copy.wait_recv()
    both = igs[:, core] + core_got[...]
    core_got[...] = both
    chip_sent[...] = both.astype(BF16)
    for i, (dy, dx) in enumerate(steps):
        chip = chip_at(dy, dx)
        go(
            remote(
                chip_sent.at[chip // 2], chip_got.at[i], d_send.at[i], d_recv.at[i], row, chip + core
            )
        )
    for g in range(1, G):
        weight_grad(g)
    done = core_got[col // 2]
    for i in reversed(range(15)):
        remote(chip_sent.at[0], chip_got.at[i], d_send.at[i], d_recv.at[i], row, col).wait_recv()
        done += chip_got[i].astype(F32)
    ig_out[...] = done.astype(BF16)

    for copy in pending:
        copy.wait_send()


def body(layer_input, out_grad, gate_weight, up_weight, down_weight):
    dma = pltpu.SemaphoreType.DMA

    def rings(late, first, late_kind, first_kind):
        return [
            pltpu.VMEM((*first, 3, 16, w), first_kind) if f else pltpu.VMEM((*late, 3, 32, w), late_kind)
            for w, f in zip(WIDTHS, FIRST)
        ]

    def halves(first_kind, late_kind):
        return [
            pltpu.VMEM((8, 3, 16, w), first_kind) if f else pltpu.VMEM((2, 3, 16, w), late_kind)
            for w, f in zip(WIDTHS, FIRST)
        ]

    scratch = [
        pltpu.VMEM((256, 1024), BF16),
        pltpu.VMEM((512, 896), BF16),
        pltpu.VMEM((512, 896), BF16),
        pltpu.VMEM((896, 512), BF16),
        *rings((8,), (2, 8), F32, F32),
        *rings((2, 2), (2, 1), BF16, BF16),
        *rings((2, 2), (2, 1), BF16, BF16),
        *rings((3,), (5,), F32, F32),
        *halves(BF16, F32),
        *halves(BF16, F32),
        *[pltpu.VMEM((8, 2, 3, 16, w), BF16) for w in WIDTHS],
        pltpu.VMEM((16, 2, 8, 512), F32),
        pltpu.VMEM((16, 8, 512), F32),
        pltpu.VMEM((16, 8, 512), BF16),
        pltpu.VMEM((15, 8, 512), BF16),
        dma((5,)),
        dma((15,)),
        dma((15,)),
        dma((16,)),
        dma((16,)),
        dma((G, 2, 4)),
        dma((G, 2, 4)),
        dma((G, 8)),
        dma((G, 8)),
        dma((G, 2, 4)),
        dma((G, 2, 4)),
        dma((G, 8)),
        dma((G, 8)),
        dma((1,)),
        dma((1,)),
        dma((15,)),
        dma((15,)),
    ]
    hbm = pl.BlockSpec(memory_space=pl.ANY)
    vmem = pl.BlockSpec(memory_space=pltpu.VMEM)
    return pl.pallas_call(
        kernel,
        out_shape=(
            jax.ShapeDtypeStruct((8, 512), BF16),
            jax.ShapeDtypeStruct((896, 512), BF16),
        ),
        in_specs=[hbm] * 5,
        out_specs=(vmem, vmem),
        scratch_shapes=scratch,
        compiler_params=pltpu.CompilerParams(
            collective_id=0, has_side_effects=True, vmem_limit_bytes=53 * 1024 * 1024
        ),
        name="swiglu_back",
    )(layer_input, out_grad, gate_weight, up_weight, down_weight)


def solution(mesh):
    return jax.shard_map(
        body,
        mesh=mesh,
        in_specs=(
            P("col", "row"),
            P("col", "row"),
            P("row", "col"),
            P("row", "col"),
            P("col", "row"),
        ),
        out_specs=(P("col", "row"), P("col", "row")),
        check_vma=False,
    )
```

time: 82.8 us -> 79.5 us (0.960)
  Pallas kernels: 78.5 us -> 75.7 us
    pallas_call x1, Pallas kernels: 78.5 us -> 75.7 us  [body(): pl.pallas_call(kernel, out_shape=(jax.ShapeDtypeStruct((8, 512), BF16), j...]
    unnamed x2 -> x6, local copies, waits for them, and re-layouts: 3.46 us -> 2.91 us
where the time goes in v2:
time: 79.5 us; the launch traced here: 79.3 us
  Pallas kernels  75.7 us (95%)
  local copies, waits for them, and re-layouts  2.91 us (4%)
    pallas_call x1, Pallas kernels, body(): pl.pallas_call(kernel, out_shape=(jax.ShapeDtypeStruct((8, 512), BF16), j...  75.7 us
    unnamed x6, local copies, waits for them, and re-layouts  2.91 us

profile of v2, /device:TPU:1, one launch (start us, length us, event | category | flops | bytes accessed | tf_op | source)
XLA Modules:
  0.0 79.3 jit_solution(15326591565960385497)
XLA Ops:
  0.6 0.0 copy-start
  0.6 0.7 copy-done
  1.3 0.0 copy-start.1
  1.3 0.7 copy-done.1
  2.0 75.7 %swiglu_back.1 = (bf16[8,512]{1,0:T(8,128)(2,1)S(1)}, bf16[896,512]{1,0:T(8,128)(2,1)S(1)}) custom-call(bf16[8,512]{1,0:T(8,128)(2,1)S(1)} %copy-done, bf16[8,512]{1,0:T(8,128)(2,1)S(1)} %copy-done.1, bf16[512,896]{1,0:T(8,128)(2,1)} %wg_hbm.1, bf16[512,896]{1,0:T(8,128)(2,1)} %wu_hbm.1, bf16[896,512]{1,0:T(8,128)(2,1)} %wd_hbm.1), custom_call_target="tpu_custom_call" | custom-call | tf_op jit(solution)/shard_map/swiglu_back/pallas_call | solution.py:378
  77.7 0.6 copy.9
  78.3 0.9 %copy.10 = bf16[896,512]{1,0:T(8,128)(2,1)} copy(bf16[896,512]{1,0:T(8,128)(2,1)S(1)} %get-tuple-element.5) | data formatting | bytes 1835008
Async XLA Ops:
  0.6 0.7 copy-start
  1.3 0.7 copy-start.1

commit v3 on v2

--- a/solution.py
+++ b/solution.py
@@ -268,56 +268,80 @@
             finish(g)
     for g in range(G):
         middle(g)
-    for k in (2, 3, 4):
-        for g in range(G):
-            forward(g, k)
-    for g in range(G):
-        if SIDE[g]:
-            forward(g, 5)
-
     def gathered(g, m):
         return full[g][:, :, m].reshape(256, WIDTHS[g])
 
-    total = None
-    for g in sorted(range(G), key=lambda g: SIDE[g]):
-        if SIDE[g]:
-            for i in range(8):
-                chunk = mod8(z - i * s) if i < 5 else mod8(z + (i - 4) * s)
-                side_copy(g, i, chunk, 1 - x_lo).wait_recv()
-        else:
-            forward(g, 5)
-        w, cols = WIDTHS[g], pl.ds(OFFS[g], WIDTHS[g])
-        term = contract_last(gathered(g, 1), wg[:, cols])
-        term += contract_last(gathered(g, 2), wu[:, cols])
-        total = term if total is None else total + term
-    igs[...] = total.reshape(16, 2, 8, 512)
-
-    core_copy = go(
-        remote(igs.at[:, 1 - core], core_got, c_send.at[0], c_recv.at[0], row, partner)
-    )
+    def chunk_at(d):
+        return mod8(z - d * s)
+
+    def core_copy(chunk):
+        return remote(
+            igs.at[chunk, :, 1 - core], core_got.at[chunk], c_send.at[chunk], c_recv.at[chunk], row, partner
+        )
+
+    def input_grad(distances):
+        total = None
+        for g in sorted(range(G), key=lambda g: SIDE[g]):
+            w, cols = WIDTHS[g], pl.ds(OFFS[g], WIDTHS[g])
+            if SIDE[g]:
+                for d in distances:
+                    side_copy(g, d if d >= 0 else 4 - d, chunk_at(d), 1 - x_lo).wait_recv()
+            for m, weight in ((1, wg), (2, wu)):
+                left = [full[g][chunk_at(d), :, m].reshape(32, w) for d in distances]
+                term = contract_last(jnp.concatenate(left, axis=0), weight[:, cols])
+                total = term if total is None else total + term
+        for n, d in enumerate(distances):
+            igs[chunk_at(d)] = total[32 * n : 32 * n + 32].reshape(2, 2, 8, 512)
+        for d in distances:
+            go(core_copy(chunk_at(d)))
+
+    def to_owners(distances):
+        for d in distances:
+            chunk = chunk_at(d)
+            core_copy(chunk).wait_recv()
+            both = igs[chunk, :, core] + core_got[chunk]
+            core_got[chunk] = both
+            chip_sent[chunk] = both.astype(BF16)
+            for half in (0, 1):
+                i = mod8(chunk - y) * 2 + lax.rem(half + x_hi, 2)
+
+                @pl.when(i != 0)
+                def _():
+                    remote(
+                        chip_sent.at[chunk, half],
+                        chip_got.at[i],
+                        d_send.at[i],
+                        d_recv.at[i],
+                        row,
+                        chunk * 4 + half * 2 + core,
+                    ).start()
 
     def weight_grad(g):
         w, cols = WIDTHS[g], pl.ds(OFFS[g], WIDTHS[g])
         dg_out[cols, :] = contract_first(gathered(g, 0), grads).astype(BF16)
 
+    for k in (2, 3):
+        for g in range(G):
+            forward(g, k)
+    input_grad((0, 1, -1))
+    for g in range(G):
+        forward(g, 4)
+    input_grad((2, -2))
+    to_owners((0, 1, -1))
+    for g in range(G):
+        forward(g, 5)
+    to_owners((2, -2))
+    input_grad((3, -3, 4))
     weight_grad(0)
-    core_copy.wait_recv()
-    both = igs[:, core] + core_got[...]
-    core_got[...] = both
-    chip_sent[...] = both.astype(BF16)
-    for i, (dy, dx) in enumerate(steps):
-        chip = chip_at(dy, dx)
-        go(
-            remote(
-                chip_sent.at[chip // 2], chip_got.at[i], d_send.at[i], d_recv.at[i], row, chip + core
-            )
-        )
+    to_owners((3, -3, 4))
     for g in range(1, G):
         weight_grad(g)
-    done = core_got[col // 2]
-    for i in reversed(range(15)):
-        remote(chip_sent.at[0], chip_got.at[i], d_send.at[i], d_recv.at[i], row, col).wait_recv()
+    done = core_got[y, x_hi]
+    for i in range(15, 0, -1):
+        owner_copy = remote(chip_sent.at[0, 0], chip_got.at[i], d_send.at[i], d_recv.at[i], row, partner)
+        owner_copy.wait_recv()
         done += chip_got[i].astype(F32)
+        pending.append(owner_copy)
     ig_out[...] = done.astype(BF16)
 
     for copy in pending:
@@ -351,10 +375,10 @@
         *halves(BF16, F32),
         *halves(BF16, F32),
         *[pltpu.VMEM((8, 2, 3, 16, w), BF16) for w in WIDTHS],
-        pltpu.VMEM((16, 2, 8, 512), F32),
-        pltpu.VMEM((16, 8, 512), F32),
+        pltpu.VMEM((8, 2, 2, 8, 512), F32),
+        pltpu.VMEM((8, 2, 8, 512), F32),
+        pltpu.VMEM((8, 2, 8, 512), BF16),
         pltpu.VMEM((16, 8, 512), BF16),
-        pltpu.VMEM((15, 8, 512), BF16),
         dma((5,)),
         dma((15,)),
         dma((15,)),
@@ -368,13 +392,15 @@
         dma((G, 2, 4)),
         dma((G, 8)),
         dma((G, 8)),
-        dma((1,)),
-        dma((1,)),
-        dma((15,)),
-        dma((15,)),
+        dma((8,)),
+        dma((8,)),
+        dma((16,)),
+        dma((16,)),
     ]
-    hbm = pl.BlockSpec(memory_space=pl.ANY)
+    hbm = pl.BlockSpec(memory_space=pltpu.HBM)
     vmem = pl.BlockSpec(memory_space=pltpu.VMEM)
+    layer_input = pltpu.with_memory_space_constraint(layer_input, pltpu.HBM)
+    out_grad = pltpu.with_memory_space_constraint(out_grad, pltpu.HBM)
     return pl.pallas_call(
         kernel,
         out_shape=(

time: 79.5 us -> 76.5 us (0.962)
  the two profiles are of different devices: /device:TPU:1 before, /device:TPU:25 now
where the time goes in v3:
time: 76.5 us; the launch traced here: 76.4 us
  Pallas kernels  74.3 us (97%)
  local copies, waits for them, and re-layouts  1.52 us (2%)
    pallas_call x1, Pallas kernels, body(): pl.pallas_call(kernel, out_shape=(jax.ShapeDtypeStruct((8, 512), BF16), j...  74.3 us

profile of v3, /device:TPU:25, one launch (start us, length us, event | category | flops | bytes accessed | tf_op | source)
XLA Modules:
  0.0 76.4 jit_solution(6439859010075566408)
XLA Ops:
  0.6 74.3 %swiglu_back.1 = (bf16[8,512]{1,0:T(8,128)(2,1)S(1)}, bf16[896,512]{1,0:T(8,128)(2,1)S(1)}) custom-call(bf16[8,512]{1,0:T(8,128)(2,1)} %li.1, bf16[8,512]{1,0:T(8,128)(2,1)} %og.1, bf16[512,896]{1,0:T(8,128)(2,1)} %wg_hbm.1, bf16[512,896]{1,0:T(8,128)(2,1)} %wu_hbm.1, bf16[896,512]{1,0:T(8,128)(2,1)} %wd_hbm.1), custom_call_target="tpu_custom_call" | custom-call | tf_op jit(solution)/shard_map/swiglu_back/pallas_call | solution.py:404
  74.9 0.6 copy.9
  75.5 0.9 %copy.10 = bf16[896,512]{1,0:T(8,128)(2,1)} copy(bf16[896,512]{1,0:T(8,128)(2,1)S(1)} %get-tuple-element.5) | data formatting | bytes 1835008

commit v4 on v3

--- a/solution.py
+++ b/solution.py
@@ -55,7 +55,7 @@
     xrecv = take(G)
     full = take(G)
     (igs, core_got, chip_sent, chip_got) = take(4)
-    (local_sem, a_send, a_recv, f_send, f_recv) = take(5)
+    (local_sem, a_send, a_recv, q_send, q_recv, f_send, f_recv) = take(7)
     (rs_send, rs_recv, x_send, x_recv, ag_send, ag_recv, side_send, side_recv) = take(8)
     (c_send, c_recv, d_send, d_recv) = take(4)
 
@@ -73,8 +73,6 @@
     across = (1 - x_lo) * NZ + z
     partner = col + s
 
-    steps = [(dy, dx) for dy in (4, 3, 5, 2, 6, 1, 7, 0) for dx in (1, 0)][:-1]
-
     def chip_at(dy, dx):
         return mod8(y + dy) * 4 + lax.rem(x_hi + dx, 2) * 2
 
@@ -93,8 +91,8 @@
         load.start()
 
     barrier = pltpu.get_barrier_semaphore()
-    greet = [(row, chip_at(dy, dx) + core) for dy, dx in steps]
-    greet += [(row, partner), (ahead, col), (behind, col), (across, col)]
+    greet = [(row, chip_at(dy, 0) + core) for dy in (2, -2, 1, -1)]
+    greet += [(row, chip_at(0, 1) + core), (row, partner), (ahead, col), (behind, col), (across, col)]
     for r, c in greet:
         pl.semaphore_signal(
             barrier, inc=1, device_id={"row": r, "col": c}, device_id_type=MESH
@@ -111,23 +109,82 @@
     def rows_of(c):
         return xg.at[pl.ds(pl.multiple_of(c * 8, 8), 8), :]
 
+    pair = chip_at(0, 1) + core
+
+    def y_copy(source, to):
+        c = chip_at(source, 0) + core
+        ahead_y = chip_at(source + to, 0) + core
+        return remote(rows_of(c), rows_of(c), a_send.at[to % 8], a_recv.at[to % 8], row, ahead_y)
+
+    def q_copy(dy, c):
+        return remote(rows_of(c), rows_of(c), q_send.at[dy % 8], q_recv.at[dy % 8], row, pair)
+
+    def f_copy(dx, dy, c):
+        return remote(rows_of(c), rows_of(c), f_send.at[dx, dy % 8], f_recv.at[dx, dy % 8], row, partner)
+
     loads[0].wait()
     loads[1].wait()
-    for i, (dy, dx) in enumerate(steps):
-        go(remote(rows_of(col), rows_of(col), a_send.at[i], a_recv.at[i], row, chip_at(dy, dx) + core))
-    go(remote(rows_of(col), rows_of(col), f_send.at[15], f_recv.at[15], row, partner))
-    for i in reversed(range(15)):
-        dy, dx = steps[i]
-        src = chip_at(-dy, dx)
-        remote(rows_of(src + core), rows_of(src + core), a_send.at[i], a_recv.at[i], row, col).wait_recv()
-        go(remote(rows_of(src + core), rows_of(src + core), f_send.at[i], f_recv.at[i], row, partner))
-    for i in reversed(range(16)):
-        src = chip_at(-steps[i][0], steps[i][1]) + 1 - core if i < 15 else partner
-        remote(rows_of(src), rows_of(src), f_send.at[i], f_recv.at[i], row, partner).wait_recv()
+    for to in (2, -2, 1, -1):
+        go(y_copy(0, to))
+    go(q_copy(0, col))
+    go(f_copy(0, 0, col))
+    def products(g, sources):
+        w, cols = WIDTHS[g], pl.ds(OFFS[g], WIDTHS[g])
+        chunks = [mod8(y + dy) for dy in sources]
+
+        def rows(columns):
+            blocks = [xg[pl.ds(pl.multiple_of(32 * c, 32), 32), columns] for c in chunks]
+            return jnp.concatenate(blocks, axis=0)
+
+        for m in range(3):
+            if m == 2:
+                value = contract_last(rows(slice(512, 1024)), wd[cols, :])
+            else:
+                value = jnp.dot(rows(slice(0, 512)), (wg, wu)[m][:, cols], preferred_element_type=F32)
+            for n, c in enumerate(chunks):
+                if FIRST[g]:
+                    part[g][0, c, m] = value[32 * n : 32 * n + 16]
+                    part[g][1, c, m] = value[32 * n + 16 : 32 * n + 32]
+                else:
+                    part[g][c, m] = value[32 * n : 32 * n + 32]
+
+    def y_arrives(to):
+        c = chip_at(-to, 0) + core
+        y_copy(-to, to).wait_recv()
+        if to == 2:
+            go(y_copy(-2, 4))
+            go(y_copy(-2, 3))
+        if to == -2:
+            go(y_copy(2, -3))
+        go(q_copy(to, c))
+        go(f_copy(0, to, c))
+
+    def q_arrives(to):
+        c = chip_at(-to, 1) + core
+        q_copy(to, c).wait_recv()
+        go(f_copy(1, to, c))
+
+    def f_arrive(to):
+        for dx in (0, 1):
+            f_copy(dx, to, chip_at(-to, dx) + 1 - core).wait_recv()
+
+    near, far = (0, 1, -1, 2, -2), (3, -3, 4)
+    for to in near[1:]:
+        y_arrives(to)
+    for to in near:
+        q_arrives(to)
+    for to in far:
+        y_arrives(to)
     for load in loads[2:]:
         load.wait()
-
-    tokens = xg[:, 0:512]
+    for to in near:
+        f_arrive(to)
+    for g in range(G):
+        products(g, near)
+    for to in far:
+        q_arrives(to)
+    for to in far:
+        f_arrive(to)
     grads = xg[:, 512:1024]
 
     def part_ref(g, chunk):
@@ -153,20 +210,6 @@
         if k <= e:
             return got16[g][flow, k - 1].astype(F32)
         return got32[g][(k - e - 1) + flow * (4 - e)]
-
-    def products(g):
-        w, cols = WIDTHS[g], pl.ds(OFFS[g], WIDTHS[g])
-        for m in range(3):
-            if m == 2:
-                value = contract_last(grads, wd[cols, :])
-            else:
-                value = jnp.dot(tokens, (wg, wu)[m][:, cols], preferred_element_type=F32)
-            if FIRST[g]:
-                value = value.reshape(8, 2, 16, w)
-                part[g][0, :, m] = value[:, 0]
-                part[g][1, :, m] = value[:, 1]
-            else:
-                part[g][:, m] = value.reshape(8, 32, w)
 
     def ring_stage(g, k):
         for flow in (0, 1):
@@ -197,7 +240,7 @@
 
     later = [g for g in range(G) if not FIRST[g]] + [g for g in range(G) if FIRST[g]]
     for g in range(G):
-        products(g)
+        products(g, far)
         if FIRST[g]:
             pair_stage(g)
         else:
@@ -380,10 +423,12 @@
         pltpu.VMEM((8, 2, 8, 512), BF16),
         pltpu.VMEM((16, 8, 512), BF16),
         dma((5,)),
-        dma((15,)),
-        dma((15,)),
-        dma((16,)),
-        dma((16,)),
+        dma((8,)),
+        dma((8,)),
+        dma((8,)),
+        dma((8,)),
+        dma((2, 8)),
+        dma((2, 8)),
         dma((G, 2, 4)),
         dma((G, 2, 4)),
         dma((G, 8)),

time: 76.5 us -> 75.1 us (0.982)
  the two profiles are of different devices: /device:TPU:25 before, /device:TPU:41 now
where the time goes in v4:
time: 75.1 us; the launch traced here: 75 us
  Pallas kernels  72.8 us (97%)
  local copies, waits for them, and re-layouts  1.52 us (2%)
    pallas_call x1, Pallas kernels, body(): pl.pallas_call(kernel, out_shape=(jax.ShapeDtypeStruct((8, 512), BF16), j...  72.8 us
    unnamed x2, local copies, waits for them, and re-layouts  1.52 us

profile of v4, /device:TPU:41, one launch (start us, length us, event | category | flops | bytes accessed | tf_op | source)
XLA Modules:
  0.0 75.0 jit_solution(2672467943817323165)
XLA Ops:
  0.6 72.8 %swiglu_back.1 = (bf16[8,512]{1,0:T(8,128)(2,1)S(1)}, bf16[896,512]{1,0:T(8,128)(2,1)S(1)}) custom-call(bf16[8,512]{1,0:T(8,128)(2,1)} %li.1, bf16[8,512]{1,0:T(8,128)(2,1)} %og.1, bf16[512,896]{1,0:T(8,128)(2,1)} %wg_hbm.1, bf16[512,896]{1,0:T(8,128)(2,1)} %wu_hbm.1, bf16[896,512]{1,0:T(8,128)(2,1)} %wd_hbm.1), custom_call_target="tpu_custom_call" | custom-call | tf_op jit(solution)/shard_map/swiglu_back/pallas_call | solution.py:449
  73.5 0.6 copy.9
  74.1 0.9 %copy.10 = bf16[896,512]{1,0:T(8,128)(2,1)} copy(bf16[896,512]{1,0:T(8,128)(2,1)S(1)} %get-tuple-element.5) | data formatting | bytes 1835008

commit v5 on v4

--- a/solution.py
+++ b/solution.py
@@ -10,7 +10,7 @@
 OFFS = (0, 256, 512, 768)
 G = len(WIDTHS)
 NZ = 8
-SIDE = (True, True, False, False)
+SIDE = (True, True, True, False)
 FIRST = (True, False, False, False)
 F32 = jnp.float32
 BF16 = jnp.bfloat16
@@ -171,10 +171,13 @@
     near, far = (0, 1, -1, 2, -2), (3, -3, 4)
     for to in near[1:]:
         y_arrives(to)
-    for to in near:
+    q_arrives(0)
+    for to in (1, -1):
         q_arrives(to)
     for to in far:
         y_arrives(to)
+    for to in (2, -2):
+        q_arrives(to)
     for load in loads[2:]:
         load.wait()
     for to in near:

time: 75.1 us -> 74.6 us (level)
  the two profiles are of different devices: /device:TPU:41 before, /device:TPU:31 now
where the time goes in v5:
time: 74.6 us; the launch traced here: 74.5 us
  Pallas kernels  72.3 us (97%)
  local copies, waits for them, and re-layouts  1.52 us (2%)
    pallas_call x1, Pallas kernels, body(): pl.pallas_call(kernel, out_shape=(jax.ShapeDtypeStruct((8, 512), BF16), j...  72.3 us
    unnamed x2, local copies, waits for them, and re-layouts  1.52 us

profile of v5, /device:TPU:31, one launch (start us, length us, event | category | flops | bytes accessed | tf_op | source)
XLA Modules:
  0.0 74.5 jit_solution(5747374261651880429)
XLA Ops:
  0.6 72.3 %swiglu_back.1 = (bf16[8,512]{1,0:T(8,128)(2,1)S(1)}, bf16[896,512]{1,0:T(8,128)(2,1)S(1)}) custom-call(bf16[8,512]{1,0:T(8,128)(2,1)} %li.1, bf16[8,512]{1,0:T(8,128)(2,1)} %og.1, bf16[512,896]{1,0:T(8,128)(2,1)} %wg_hbm.1, bf16[512,896]{1,0:T(8,128)(2,1)} %wu_hbm.1, bf16[896,512]{1,0:T(8,128)(2,1)} %wd_hbm.1), custom_call_target="tpu_custom_call" | custom-call | tf_op jit(solution)/shard_map/swiglu_back/pallas_call | solution.py:452
  73.0 0.6 copy.9
  73.6 0.9 %copy.10 = bf16[896,512]{1,0:T(8,128)(2,1)} copy(bf16[896,512]{1,0:T(8,128)(2,1)S(1)} %get-tuple-element.5) | data formatting | bytes 1835008
